TPU v7x, 128 devices: a whole 4x4x4 slice. The times are simulated.
128 devices in a mesh: dy: 4 (over x), dx: 32 (over z, y, core).
Axes of the slice: x: 4, y: 4, z: 4, core: 2. Of those that a mesh axis runs over, the one named last changes fastest.
Arguments:
- tokens: bfloat16 [32768, 1024], P(('dy', 'dx'))
- targets: bfloat16 [32768, 1024], P(('dy', 'dx'))
- w_in: bfloat16 [4, 1024, 4096], replicated
- w_out: bfloat16 [4, 4096, 1024], replicated
Outputs:
- output 1: float32 [4, 1024, 4096], replicated
- output 2: float32 [4, 4096, 1024], replicated
All inputs are finite; a program needn't handle non-finite values.
Results may differ from a plain program's by a relative error of at most 0.00957852.
Values are sent between devices in bfloat16 or wider.
A program may use at most 1 GiB of HBM per device.

v0:
```python
import jax
import jax.numpy as jnp
from jax import lax
from jax.sharding import PartitionSpec as P

DATA_AXES = ('dy', 'dx')
ROW_CONTRACT = (((0,), (0,)), ((), ()))
COL_CONTRACT = (((1,), (1,)), ((), ()))


def forward_stack(tokens, w_in, w_out):
    hidden = tokens
    saved = []
    for layer in range(w_in.shape[0]):
        pre_act = jnp.dot(hidden, w_in[layer], preferred_element_type=jnp.float32).astype(jnp.bfloat16)
        post_act = jax.nn.gelu(pre_act.astype(jnp.float32)).astype(jnp.bfloat16)
        saved.append((hidden, pre_act, post_act))
        branch = jnp.dot(post_act, w_out[layer], preferred_element_type=jnp.float32)
        hidden = (hidden.astype(jnp.float32) + branch).astype(jnp.bfloat16)
    return hidden, saved


def layer_backward(grad_hid, hidden, pre_act, post_act, w_second):
    grad_w_out = lax.dot_general(post_act, grad_hid, ROW_CONTRACT, preferred_element_type=jnp.float32)
    grad_post = lax.dot_general(grad_hid, w_second, COL_CONTRACT, preferred_element_type=jnp.float32)
    gelu_vjp = jax.vjp(jax.nn.gelu, pre_act.astype(jnp.float32))[1]
    grad_pre = gelu_vjp(grad_post)[0].astype(jnp.bfloat16)
    grad_w_in = lax.dot_general(hidden, grad_pre, ROW_CONTRACT, preferred_element_type=jnp.float32)
    return grad_w_in, grad_w_out, grad_pre


def input_grad(grad_hid, grad_pre, w_first):
    through_w = lax.dot_general(grad_pre, w_first, COL_CONTRACT, preferred_element_type=jnp.float32)
    return (grad_hid.astype(jnp.float32) + through_w).astype(jnp.bfloat16)


def solution(mesh):
    def run(tokens, targets, w_in, w_out):
        inv_total = 1.0 / tokens.shape[0]

        def local_step(tok_local, tgt_local, w_first_all, w_second_all):
            final, saved = forward_stack(tok_local, w_first_all, w_second_all)
            grad_hid = ((final.astype(jnp.float32) - tgt_local.astype(jnp.float32)) * inv_total).astype(jnp.bfloat16)
            num_layers = w_first_all.shape[0]
            grads_in = [None] * num_layers
            grads_out = [None] * num_layers
            for layer in reversed(range(num_layers)):
                hidden, pre_act, post_act = saved[layer]
                grad_w_in, grad_w_out, grad_pre = layer_backward(grad_hid, hidden, pre_act, post_act, w_second_all[layer])
                grads_in[layer], grads_out[layer] = lax.psum((grad_w_in, grad_w_out), DATA_AXES)
                if layer > 0:
                    grad_hid = input_grad(grad_hid, grad_pre, w_first_all[layer])
            return jnp.stack(grads_in), jnp.stack(grads_out)

        data_spec = P(DATA_AXES, None)
        mapped = jax.shard_map(local_step, mesh=mesh, in_specs=(data_spec, data_spec, P(), P()), out_specs=(P(), P()), check_vma=False)
        return mapped(tokens, targets, w_in, w_out)

    return run
```

profile of v0, /device:TPU:1, one launch (start us, length us, event | category | flops | bytes accessed | tf_op | source)
XLA Modules:
  0.0 1126.5 jit_solution(7644655323774186741)
XLA Ops:
  7.2 0.0 all-reduce.6.cloned.1.call-start
  7.2 5.9 fusion.49
  13.2 6.2 fusion.158
  19.4 5.7 fusion.52
  25.1 6.2 fusion.152
  31.3 5.7 fusion.55
  37.1 6.6 fusion.146
  43.6 0.0 copy-start
  43.7 5.8 fusion.58
  49.4 6.3 fusion.140
  55.7 6.9 fusion.63
  62.7 5.7 fusion.143
  68.4 6.9 fusion.66
  75.4 5.7 fusion.149
  81.1 7.1 fusion.69
  88.2 8.9 convolution_bitcast_fusion.2
  97.1 5.7 fusion.155
  102.8 8.1 convolution_bitcast_fusion.6
  110.9 8.5 convolution_bitcast_fusion.5
  119.5 8.7 convolution_bitcast_fusion.1
  128.2 8.9 convolution_bitcast_fusion
  137.1 8.5 convolution_bitcast_fusion.4
  145.7 11.9 %convolution_bitcast_fusion.7 = f32[1,1024,4096]{1,2,0:T(8,128)} fusion(bf16[256,1024]{1,0:T(8,128)(2,1)S(1)} %copy-done.1, bf16[256,4096]{1,0:T(8,128)(2,1)S(1)} %fusion.49, bf16[256,1024]{1,0:T(8,128)(2,1)S(1)} %fusion.155, bf16[4,4096,1024]{2,1,0:T(8,128)(2,1)} %param.7), kind=kOutput, calls=%fused_computation.9 | convolution fusion | flops 4316987392 | bytes 28311552 | tf_op jit(solution)/shard_map/dot_general | solution.py:28
  157.5 0.0 all-reduce.6.cloned.1.call-update
  157.6 0.0 all-reduce.4.cloned.1.call-start
  157.6 8.8 convolution_bitcast_fusion.3
  166.4 0.0 all-reduce.4.cloned.1.call-update
  166.5 687.0 %all-reduce.6.cloned.1.call-done = (f32[1,1024,4096]{1,2,0:T(8,128)}, f32[1,1024,4096]{1,2,0:T(8,128)}, f32[1,1024,4096]{1,2,0:T(8,128)}, f32[1,1024,4096]{1,2,0...) async-done(((f32[1,1024,4096]{1,2,0:T(8,128)}, f32[1,1024,4096]{1,2,0:T(8,128)}, f32[1,1024,4096]{1,2,0:T(8,128)}, ...) | async-done | bytes 117440528 | tf_op jit(solution)/shard_map/psum | solution.py:50
  853.5 45.6 %pad_maximum_fusion = f32[4,1024,4096]{1,2,0:T(8,128)} fusion(f32[1,1024,4096]{1,2,0:T(8,128)} %get-tuple-element.4, f32[1,1024,4096]{1,2,0:T(8,128)} %get-tuple-element.5, f32[1,1024,4096]{1,2,0:T(8,128)} %get-tuple-element.6, f32[1,1024,4096]{1,2,0:T(8,128)} %get-tuple-element.7), kind=kLoop, calls=%fused_computation | loop fusion | flops 50331648 | bytes 134217728 | tf_op jit(solution)/shard_map/stack | solution.py:53
  899.0 62.0 %copy.9 = f32[4,1024,4096]{2,1,0:T(8,128)} copy(f32[4,1024,4096]{1,2,0:T(8,128)} %pad_maximum_fusion) | data formatting | bytes 134217728
  961.0 114.0 %all-reduce.4.cloned.1.call-done = f32[1,4096,1024]{2,1,0:T(8,128)} async-done(((f32[1,4096,1024]{2,1,0:T(8,128)}), f32[1,4096,1024]{2,1,0:T(8,128)}) %all-reduce.4.cloned.1.call-update) | async-done | bytes 16777232 | tf_op jit(solution)/shard_map/psum | solution.py:50
  1075.0 44.3 %pad_maximum_fusion.1 = f32[4,4096,1024]{2,1,0:T(8,128)} fusion(f32[1,4096,1024]{2,1,0:T(8,128)} %get-tuple-element.8, f32[1,4096,1024]{2,1,0:T(8,128)} %get-tuple-element.9, f32[1,4096,1024]{2,1,0:T(8,128)} %get-tuple-element.10, f32[1,4096,1024]{2,1,0:T(8,128)} %all-reduce.4.cloned.1.call-done), kind=kLoop, calls=%fused_computation.1 | loop fusion | flops 50331648 | bytes 134217728 | tf_op jit(solution)/shard_map/stack | solution.py:53
  (3 shorter events, 0.0 us)
Async XLA Ops:
  7.2 6.0 copy-start.1
  7.2 846.3 %all-reduce.6.cloned.1.call-start = ((), (), s32[]{:S(2)}) async-start(), calls=%async_computation.1 | async-start | bytes 234881024 | tf_op jit(solution)/shard_map/psum | solution.py:50
  43.6 5.8 copy-start
  157.6 917.4 %all-reduce.4.cloned.1.call-start = ((), (), s32[]{:S(2)}) async-start(), calls=%async_computation | async-start | bytes 33554432 | tf_op jit(solution)/shard_map/psum | solution.py:50
Sparse Core Ops, SparseCore 0:
  157.7 695.7 all-reduce.5
  858.9 215.9 all-reduce.3
where the time goes:
time: 1140 us; the launch traced here: 1130 us
  waiting for transfers between devices  801 us (70%)
  matrix products  159 us (14%)
  other arithmetic  89.8 us (8%)
  local copies, waits for them, and re-layouts  62 us (5%)
  between operations  14.6 us (1%)
    psum x2, waiting for transfers between devices, local_step(): lax.psum((grad_w_in, grad_w_out), DATA_AXES)  801 us
    another operation x2, other arithmetic, local_step(): return (jnp.stack(grads_in), jnp.stack(grads_out))  89.8 us
    unnamed x5, local copies, waits for them, and re-layouts  62 us
    dot_general x4, matrix products, layer_backward(): lax.dot_general(hidden, grad_pre, ROW_CONTRACT, preferred_element_type=jn...  37.1 us
    dot_general x4, matrix products, layer_backward(): lax.dot_general(post_act, grad_hid, ROW_CONTRACT, preferred_element_type=...  35.3 us
    dot_general x4, matrix products, forward_stack(): branch = jnp.dot(post_act, w_out[layer], preferred_element_type=jnp.float32)  25.3 us
    dot_general x4, matrix products, forward_stack(): jnp.dot(hidden, w_in[layer], preferred_element_type=jnp.float32)  23.2 us
  transfers between devices with their start and end apart: 2, of which 2 were waited for; matrix products, arithmetic and copies ran while one was open for 10% of the time, Pallas kernels for 0%

commit v1 on v0

v1 whole, which is shorter than its diff:
```python
import functools

import jax
import jax.numpy as jnp
from jax import lax
from jax.experimental import pallas as pl
from jax.experimental.pallas import tpu as pltpu
from jax.sharding import PartitionSpec as P

DATA_AXES = ('dy', 'dx')
MESH = pl.DeviceIdType.MESH
RING = 4
ROW_CONTRACT = (((0,), (0,)), ((), ()))
COL_CONTRACT = (((1,), (1,)), ((), ()))
F32, BF16 = jnp.float32, jnp.bfloat16


def local_pass(tokens, targets, w_in, w_out, inv_total):
    rows, dim = tokens.shape
    layers, _, hid = w_in.shape
    width = min(1024, hid)
    tiles = hid // width

    def body(tok, tgt, w1, w2, h_out, a_out, p_out, g_out, cur, acc, pre):
        step, tile = pl.program_id(0), pl.program_id(1)
        first, last = tile == 0, tile == tiles - 1

        def add(term):
            @pl.when(first)
            def _():
                acc[...] = term

            @pl.when(tile > 0)
            def _():
                acc[...] += term

        @pl.when((step == 0) & first)
        def _():
            cur[...] = tok[...]

        @pl.when(step < layers)
        def _():
            @pl.when(first)
            def _():
                h_out[...] = cur[...]

            pre_act = jnp.dot(cur[...], w1[...], preferred_element_type=F32).astype(BF16)
            pre[step, tile] = pre_act
            post_act = jax.nn.gelu(pre_act.astype(F32)).astype(BF16)
            a_out[...] = post_act
            add(jnp.dot(post_act, w2[...], preferred_element_type=F32))

            @pl.when(last)
            def _():
                cur[...] = (cur[...].astype(F32) + acc[...]).astype(BF16)

        @pl.when((step == layers - 1) & last)
        def _():
            cur[...] = ((cur[...].astype(F32) - tgt[...].astype(F32)) * inv_total).astype(BF16)

        @pl.when(step >= layers)
        def _():
            @pl.when(first)
            def _():
                g_out[...] = cur[...]

            grad_post = lax.dot_general(cur[...], w2[...], COL_CONTRACT, preferred_element_type=F32)
            pre_act = pre[2 * layers - 1 - step, tile].astype(F32)
            grad_pre = jax.vjp(jax.nn.gelu, pre_act)[1](grad_post)[0].astype(BF16)
            p_out[...] = grad_pre

            @pl.when(step < 2 * layers - 1)
            def _():
                add(lax.dot_general(grad_pre, w1[...], COL_CONTRACT, preferred_element_type=F32))

                @pl.when(last)
                def _():
                    cur[...] = (cur[...].astype(F32) + acc[...]).astype(BF16)

    top = layers - 1

    def layer_of(step):
        return jnp.where(step < layers, step, 2 * layers - 1 - step)

    def w1_at(step, tile):
        spare = step == 2 * layers - 1
        return jnp.where(spare, min(1, top), layer_of(step)), 0, jnp.where(spare, tiles - 1, tile)

    def fwd_at(step, tile):
        return jnp.minimum(step, top), 0, jnp.where(step < layers, tile, tiles - 1)

    def bwd_at(step, tile):
        return jnp.minimum(2 * layers - 1 - step, top), 0, jnp.where(step < layers, 0, tile)

    whole = pl.BlockSpec((rows, dim), lambda step, tile: (0, 0))
    return pl.pallas_call(
        body,
        grid=(2 * layers, tiles),
        in_specs=[
            whole,
            whole,
            pl.BlockSpec((None, dim, width), w1_at),
            pl.BlockSpec((None, width, dim), lambda step, tile: (layer_of(step), tile, 0)),
        ],
        out_specs=[
            pl.BlockSpec((None, rows, dim), lambda step, tile: (jnp.minimum(step, top), 0, 0)),
            pl.BlockSpec((None, rows, width), fwd_at),
            pl.BlockSpec((None, rows, width), bwd_at),
            pl.BlockSpec((None, rows, dim), lambda step, tile: (jnp.minimum(2 * layers - 1 - step, top), 0, 0)),
        ],
        out_shape=[
            jax.ShapeDtypeStruct((layers, rows, dim), BF16),
            jax.ShapeDtypeStruct((layers, rows, hid), BF16),
            jax.ShapeDtypeStruct((layers, rows, hid), BF16),
            jax.ShapeDtypeStruct((layers, rows, dim), BF16),
        ],
        scratch_shapes=[
            pltpu.VMEM((rows, dim), BF16),
            pltpu.VMEM((rows, dim), F32),
            pltpu.VMEM((layers, tiles, rows, width), BF16),
        ],
        compiler_params=pltpu.CompilerParams(vmem_limit_bytes=56 << 20, dimension_semantics=('arbitrary', 'arbitrary')),
        cost_estimate=pl.CostEstimate(
            flops=8 * layers * rows * dim * hid, bytes_accessed=8 * layers * dim * hid, transcendentals=2 * layers * rows * hid
        ),
        name='local_pass',
    )(tokens, targets, w_in, w_out)


OUT, IN = 0, 1
SHARES = ((6, 6, 4), (5, 5, 6))


class Reducer:
    def __init__(self, refs, layers, toks, dim, hid):
        (
            (self.h, self.a, self.p, self.g),
            (self.r_in, self.r_out, self.xh, self.xa, self.xp, self.xg),
            (self.lop, self.rop, self.wp, self.near, self.far),
            (self.rs_send, self.rs_recv, self.ag_send, self.ag_recv, self.pair_send, self.pair_recv, self.own_sem, self.load_sem),
            (self.x_send, self.x_recv),
        ) = refs
        self.layers, self.toks, self.half = layers, toks, hid // 2
        self.rows = (hid // 2, dim)
        cols = (dim, hid // 2)
        self.cut = []
        for kind in (OUT, IN):
            start, cuts = 0, []
            for share in SHARES[kind]:
                size = cols[kind] * share // 16
                cuts.append((start, size))
                start += size
            self.cut.append(cuts)
        dx = lax.axis_index('dx')
        self.core = lax.rem(dx, 2)
        self.at = (lax.axis_index('dy'), lax.rem(lax.div(dx, 2), RING), lax.div(dx, 2 * RING))

    def device(self, axis=None, shift=0, core=None):
        x, y, z = (lax.rem(c + shift, RING) if i == axis else c for i, c in enumerate(self.at))
        return x, (z * RING + y) * 2 + (self.core if core is None else core)

    def partner(self):
        return self.device(core=1 - self.core)

    def cols(self, kind, part):
        start, size = self.cut[kind][part]
        return pl.ds(start, size)

    def span(self, kind, part, phase, block, half=None):
        size = self.rows[kind] // RING
        base = 0
        for earlier in range(phase):
            base = base + self.at[(part + earlier) % 3] * size
            size //= RING
        row = base + lax.rem(self.at[(part + phase) % 3] + block, RING) * size
        if half is not None:
            size //= 2
            row = row + half * size
        return pl.multiple_of(row, size), size

    def result(self, kind, layer, part, row, size):
        start, width = self.cut[kind][part]
        if kind == OUT:
            return self.r_out.at[layer, pl.ds(pl.multiple_of(self.core * self.half + row, size), size), pl.ds(start, width)]
        col = pl.multiple_of(self.core * self.half + start, width if self.half % width == 0 else min(128, width))
        return self.r_in.at[layer, pl.ds(row, size), pl.ds(col, width)]


    def swap(self, kind, layer, j):
        theirs = pl.ds(pl.multiple_of((1 - self.core) * self.half, self.half), self.half)
        src, dst = (
            ((self.a.at[layer, :, theirs], self.xa.at[layer]), (self.g.at[layer], self.xg.at[layer])),
            ((self.h.at[layer], self.xh.at[layer]), (self.p.at[layer, :, theirs], self.xp.at[layer])),
        )[kind][j]
        return pltpu.make_async_remote_copy(
            src, dst, self.x_send.at[layer, kind, j], self.x_recv.at[layer, kind, j], device_id=self.partner(), device_id_type=MESH
        )

    def loads(self, kind, layer):
        mine = pl.ds(pl.multiple_of(self.core * self.half, self.half), self.half)
        own, other = pl.ds(0, self.toks), pl.ds(self.toks, self.toks)
        lop, rop, sem = self.lop[kind], self.rop[kind], self.load_sem[kind]
        first, second = (
            ((self.a.at[layer, :, mine], self.xa.at[layer]), (self.g.at[layer], self.xg.at[layer])),
            ((self.h.at[layer], self.xh.at[layer]), (self.p.at[layer, :, mine], self.xp.at[layer])),
        )[kind]
        return [
            pltpu.make_async_copy(first[0], lop.at[own], sem.at[0]),
            pltpu.make_async_copy(first[1], lop.at[other], sem.at[1]),
            pltpu.make_async_copy(second[0], rop.at[own], sem.at[2]),
            pltpu.make_async_copy(second[1], rop.at[other], sem.at[3]),
        ]

    def load(self, kind, layer):
        for j in range(2):
            self.swap(kind, layer, j).wait_recv()
        for copy in self.loads(kind, layer):
            copy.start()

    def product(self, kind, layer):
        for copy in self.loads(kind, layer):
            copy.wait()
        lop, rop, wp = self.lop[kind], self.rop[kind], self.wp[kind]
        block = min(256, self.rows[kind])

        def step(b, carry):
            rows = pl.ds(pl.multiple_of(b * block, block), block)
            wp[rows, :] = lax.dot_general(lop[:, rows], rop[...], ROW_CONTRACT, preferred_element_type=F32)
            return carry

        lax.fori_loop(0, self.rows[kind] // block, step, 0)


    def rs(self, kind, part, phase, step, way):
        if step == 0:
            row, size = self.span(kind, part, phase, 2, way)
            dst = self.near[kind][phase]
        else:
            row, size = self.span(kind, part, phase, 1 if way == 0 else 3)
            dst = self.far[kind][phase]
        cols = self.cols(kind, part)
        index = (part, phase, step, way)
        return pltpu.make_async_remote_copy(
            self.wp[kind].at[pl.ds(row, size), cols],
            dst.at[way, :, cols],
            self.rs_send[kind].at[index],
            self.rs_recv[kind].at[index],
            device_id=self.device((part + phase) % 3, 1 if way == 0 else 3),
            device_id_type=MESH,
        )

    def accumulate(self, kind, part, row, size, sources):
        cols = self.cols(kind, part)
        chunk = min(8, size)

        def step(i, carry):
            at = pl.multiple_of(i * chunk, chunk)
            here = pl.ds(pl.multiple_of(row + at, chunk), chunk)
            total = self.wp[kind][here, cols]
            for ref, slot in sources:
                total = total + ref[slot, pl.ds(at, chunk), cols]
            self.wp[kind][here, cols] = total
            return carry

        lax.fori_loop(0, size // chunk, step, 0)

    def reduce_1(self, kind, layer, phase):
        for part in range(3):
            for way in range(2):
                self.rs(kind, part, phase, 0, way).start()

    def reduce_2(self, kind, layer, phase):
        for part in range(3):
            for way in range(2):
                self.rs(kind, part, phase, 0, way).wait_recv()
                row, size = self.span(kind, part, phase, 1 if way == 0 else 3, way)
                self.accumulate(kind, part, row, size, [(self.near[kind][phase], way)])
                self.rs(kind, part, phase, 1, way).start()

    def reduce_3(self, kind, layer, phase):
        for part in range(3):
            for way in range(2):
                self.rs(kind, part, phase, 1, way).wait_recv()
            row, size = self.span(kind, part, phase, 0)
            self.accumulate(kind, part, row, size, [(self.far[kind][phase], 0), (self.far[kind][phase], 1)])
            for way in range(2):
                if phase < 2:
                    self.rs(kind, part, phase + 1, 0, way).start()
                else:
                    self.ag(kind, layer, part, 2, 0, way).start()
            if phase == 2:
                self.keep(kind, layer, part).start()


    def keep(self, kind, layer, part):
        row, size = self.span(kind, part, 2, 0)
        src = self.wp[kind].at[pl.ds(row, size), self.cols(kind, part)]
        return pltpu.make_async_copy(src, self.result(kind, layer, part, row, size), self.own_sem[kind].at[part])

    def ag(self, kind, layer, part, phase, step, way):
        if step == 0:
            row, size = self.span(kind, part, phase, 0)
        else:
            row, size = self.span(kind, part, phase, 3 if way == 0 else 1, way)
        dst = self.result(kind, layer, part, row, size)
        src = self.wp[kind].at[pl.ds(row, size), self.cols(kind, part)] if (phase, step) == (2, 0) else dst
        index = (part, phase, step, way)
        return pltpu.make_async_remote_copy(
            src,
            dst,
            self.ag_send[kind].at[index],
            self.ag_recv[kind].at[index],
            device_id=self.device((part + phase) % 3, 1 if way == 0 else 3),
            device_id_type=MESH,
        )

    def pair(self, kind, layer, part, j):
        block, half = ((0, None), (3, None), (1, None), (2, 0), (2, 1))[j]
        row, size = self.span(kind, part, 0, block, half)
        ref = self.result(kind, layer, part, row, size)
        return pltpu.make_async_remote_copy(
            ref, ref, self.pair_send[kind].at[part, j], self.pair_recv[kind].at[part, j], device_id=self.partner(), device_id_type=MESH
        )

    def gather_1(self, kind, layer, phase):
        for part in range(3):
            for way in range(2):
                self.ag(kind, layer, part, phase + 1, 1, way).wait_recv()
            if phase == 1:
                self.keep(kind, layer, part).wait()
            for way in range(2):
                self.ag(kind, layer, part, phase, 0, way).start()
            if phase == 0:
                self.pair(kind, layer, part, 0).start()

    def gather_2(self, kind, layer, phase):
        for part in range(3):
            for way in range(2):
                self.ag(kind, layer, part, phase, 0, way).wait_recv()
                self.ag(kind, layer, part, phase, 1, way).start()
                if phase == 0:
                    self.pair(kind, layer, part, 1 + way).start()

    def gather_3(self, kind, layer):
        for part in range(3):
            for way in range(2):
                self.ag(kind, layer, part, 0, 1, way).wait_recv()
                self.pair(kind, layer, part, 3 + way).start()

    def finish(self, kind, layer):
        for part in range(3):
            for phase in range(3):
                for step in range(2):
                    for way in range(2):
                        self.rs(kind, part, phase, step, way).wait_send()
                        self.ag(kind, layer, part, phase, step, way).wait_send()
            for j in range(5):
                self.pair(kind, layer, part, j).wait()


    def meet(self):
        barrier = pltpu.get_barrier_semaphore()
        others = [self.device(axis, shift) for axis in range(3) for shift in (1, 3)] + [self.partner()]
        for other in others:
            pl.semaphore_signal(barrier, inc=1, device_id=other, device_id_type=MESH)
        pl.semaphore_wait(barrier, len(others))

    def overlap(self, gathered, reduced, following):
        stages = (
            ('R', self.product),
            ('F', self.load),
            ('R', self.reduce_1, 0),
            ('G', self.gather_2, 2),
            ('G', self.gather_1, 1),
            ('R', self.reduce_2, 0),
            ('G', self.gather_2, 1),
            ('G', self.gather_1, 0),
            ('R', self.reduce_3, 0),
            ('R', self.reduce_2, 1),
            ('G', self.gather_2, 0),
            ('R', self.reduce_3, 1),
            ('R', self.reduce_2, 2),
            ('G', self.gather_3),
            ('R', self.reduce_3, 2),
            ('G', self.finish),
        )
        units = {'G': gathered, 'R': reduced, 'F': following}
        for whose, stage, *phase in stages:
            if units[whose] is not None:
                stage(*units[whose], *phase)

    def run(self):
        top = self.layers - 1
        self.meet()
        for layer in reversed(range(self.layers)):
            for kind in (OUT, IN):
                for j in range(2):
                    self.swap(kind, layer, j).start()
        self.load(OUT, top)
        self.overlap(None, (OUT, top), (IN, top))

        def step(i, carry):
            layer = top - i
            self.overlap((OUT, layer), (IN, layer), (OUT, layer - 1))
            self.overlap((IN, layer), (OUT, layer - 1), (IN, layer - 1))
            return carry

        lax.fori_loop(0, top, step, 0)
        self.overlap((OUT, 0), (IN, 0), None)
        self.overlap((IN, 0), None, None)
        for layer in reversed(range(self.layers)):
            for kind in (OUT, IN):
                for j in range(2):
                    self.swap(kind, layer, j).wait_send()


def reduce_grads(h, a, p, g):
    layers, toks, dim = h.shape
    hid = a.shape[-1]
    rows, cols = (hid // 2, dim), (dim, hid // 2)
    scratch = []
    for kind in (OUT, IN):
        block = rows[kind] // RING
        scratch += [
            pltpu.VMEM((2 * toks, rows[kind]), BF16),
            pltpu.VMEM((2 * toks, cols[kind]), BF16),
            pltpu.VMEM((rows[kind], cols[kind]), F32),
        ]
        for size in (block, block // RING, block // RING**2):
            scratch += [pltpu.VMEM((2, size // 2, cols[kind]), F32), pltpu.VMEM((2, size, cols[kind]), F32)]
    sems = [pltpu.SemaphoreType.DMA((3, 3, 2, 2))] * 4 + [pltpu.SemaphoreType.DMA((3, 5))] * 2
    sems += [pltpu.SemaphoreType.DMA((3,)), pltpu.SemaphoreType.DMA((4,))]
    scratch += sems * 2 + [pltpu.SemaphoreType.DMA((layers, 2, 2))] * 2

    def body(*refs):
        ins, outs, rest = refs[:4], refs[4:10], refs[10:]
        ops = rest[:9], rest[9:18]
        lop, rop, wp = ([o[i] for o in ops] for i in range(3))
        near, far = [o[3::2] for o in ops], [o[4::2] for o in ops]
        kinds = list(zip(rest[18:26], rest[26:34]))
        Reducer((ins, outs, (lop, rop, wp, near, far), kinds, rest[34:36]), layers, toks, dim, hid).run()

    anywhere = pl.BlockSpec(memory_space=pl.ANY)
    return pl.pallas_call(
        body,
        in_specs=[anywhere] * 4,
        out_specs=[anywhere] * 6,
        out_shape=[
            jax.ShapeDtypeStruct((layers, dim, hid), F32),
            jax.ShapeDtypeStruct((layers, hid, dim), F32),
            jax.ShapeDtypeStruct((layers, toks, dim), BF16),
            jax.ShapeDtypeStruct((layers, toks, hid // 2), BF16),
            jax.ShapeDtypeStruct((layers, toks, hid // 2), BF16),
            jax.ShapeDtypeStruct((layers, toks, dim), BF16),
        ],
        scratch_shapes=scratch,
        compiler_params=pltpu.CompilerParams(collective_id=1, has_side_effects=True, vmem_limit_bytes=60 << 20),
        cost_estimate=pl.CostEstimate(flops=4 * layers * toks * dim * hid, bytes_accessed=32 * layers * dim * hid, transcendentals=0),
        name='reduce_grads',
    )(h, a, p, g)[:2]


def solution(mesh):
    def run(tokens, targets, w_in, w_out):
        inv_total = 1.0 / tokens.shape[0]

        def local_step(tok_local, tgt_local, w_first_all, w_second_all):
            return reduce_grads(*local_pass(tok_local, tgt_local, w_first_all, w_second_all, inv_total))

        data_spec = P(DATA_AXES, None)
        mapped = jax.shard_map(local_step, mesh=mesh, in_specs=(data_spec, data_spec, P(), P()), out_specs=(P(), P()), check_vma=False)
        return mapped(tokens, targets, w_in, w_out)

    return run
```

time: 1140 us -> 824 us (0.72); the launches traced: 1130 us -> 824 us
  waiting for transfers between devices: 801 us -> 0 us
  Pallas kernels: 0 us -> 736 us
  matrix products: 159 us -> 0 us
  other arithmetic: 89.8 us -> 0 us
  local copies, waits for them, and re-layouts: 62 us -> 87.8 us
  between operations: 14.6 us -> 0.64 us
    psum x2 -> x0, waiting for transfers between devices: 801 us -> none  [local_step(): lax.psum((grad_w_in, grad_w_out), DATA_AXES)]
    pallas_call x0 -> x2, Pallas kernels: none -> 736 us  [the longest x1 665 us: reduce_grads(): pl.pallas_call(body, in_specs=[anywhere] * 4, out_specs=[anywhere] * 6, o...]
    dot_general x22 -> x0, matrix products: 159 us -> none  [the longest x4 37.1 us: layer_backward(): lax.dot_general(hidden, grad_pre, ROW_CONTRACT, preferred_element_type=jn...]
    another operation x2 -> x0, other arithmetic: 89.8 us -> none  [local_step(): return (jnp.stack(grads_in), jnp.stack(grads_out))]
    unnamed x5 -> x2, local copies, waits for them, and re-layouts: 62 us -> 87.8 us
  transfers between devices with their start and end apart: 2 -> 0, of which waited for: 2 -> 0; matrix products, arithmetic and copies ran while one was open for 10% -> 0% of each run, Pallas kernels for 0% -> 0%
where the time goes in v1:
time: 824 us
  Pallas kernels  736 us (89%)
  local copies, waits for them, and re-layouts  87.8 us (11%)
    pallas_call x1, Pallas kernels, reduce_grads(): pl.pallas_call(body, in_specs=[anywhere] * 4, out_specs=[anywhere] * 6, o...  665 us
    unnamed x2, local copies, waits for them, and re-layouts  87.8 us
    pallas_call x1, Pallas kernels, local_pass(): pl.pallas_call(body, grid=(2 * layers, tiles), in_specs=[whole, whole, pl...  70.9 us

profile of v1, /device:TPU:1, one launch (start us, length us, event | category | flops | bytes accessed | tf_op | source)
XLA Modules:
  0.0 824.2 jit_solution(17080051939538322789)
XLA Ops:
  0.6 70.9 %local_pass.1 = (bf16[4,256,1024]{2,1,0:T(8,128)(2,1)}, bf16[4,256,4096]{2,1,0:T(8,128)(2,1)}, bf16[4,256,4096]{2,1,0:T(8,128)(2,1)}, bf16[4,256,1024]{2,1,0:T(8,128)(2,1)}) custom-call(bf16[256,1024]{1,0:T(8,128)(2,1)} %tok.1, bf16[256,1024]{1,0:T(8,128)(2,1)} %tgt.1, bf16[4,1024,4096]{2,1,0:T(8,128)(2,1)} %w1.1, bf16[4,4096,1024]{2,1,0:T(8,128)(2,1)} %w2.1), custom_call_target="tpu_custom_call" | custom-call | flops 34359738368 | bytes 134217728 | tf_op jit(solution)/shard_map/local_pass/pallas_call | solution.py:96
  71.5 664.9 %reduce_grads.1 = (f32[4,1024,4096]{2,1,0:T(8,128)}, f32[4,4096,1024]{2,1,0:T(8,128)}, bf16[4,256,1024]{2,1,0:T(8,128)(2,1)}, bf16[4,256,2048]{2,1,0:T(8,128)(2,...) custom-call(bf16[4,256,1024]{2,1,0:T(8,128)(2,1)} %get-tuple-element.8.refs_0_, ...), custom_call_target="tpu_custom_call" | custom-call | flops 17179869184 | bytes 536870912 | tf_op jit(solution)/shard_map/reduce_grads/pallas_call | solution.py:444
  736.4 44.2 %copy.8 = f32[4,1024,4096]{2,1,0:T(8,128)} copy(f32[4,1024,4096]{2,1,0:T(8,128)} %get-tuple-element.16) | data formatting | bytes 134217728
  780.6 43.6 %copy.9 = f32[4,4096,1024]{2,1,0:T(8,128)} copy(f32[4,4096,1024]{2,1,0:T(8,128)} %get-tuple-element.17) | data formatting | bytes 134217728
